TPU v7x, 32 devices: a whole 2x2x4 slice. The times are simulated.
32 devices in a mesh: dp: 4 (over x, y), tp: 8 (over z, core).
Axes of the slice: x: 2, y: 2, z: 4, core: 2. Of those that a mesh axis runs over, the one named last changes fastest.
Arguments:
- x: bfloat16 [512, 8192], P('dp'), parts along dimension 0
- w_gate: bfloat16 [8192, 28672], P(None, 'tp')
- w_up: bfloat16 [8192, 28672], P(None, 'tp')
- w_down: bfloat16 [28672, 8192], P('tp')
Outputs:
- output: bfloat16 [512, 8192], P('dp'), parts along dimension 0
There are 4 independent parts. A program takes and returns all parts, laid end to end along the dimension named above; an argument that names none is the same for every part.
All inputs are finite; a program needn't handle non-finite values.
Results may differ from a plain program's by a relative error of at most 0.016.
Values are sent between devices in bfloat16 or wider.
A program may use at most 2 GiB of HBM per device.

v0:
```python
import jax
import jax.numpy as jnp
from jax import lax
from jax.sharding import PartitionSpec as P


def solution(mesh):
    def step(x, w_gate, w_up, w_down):
        gate = jnp.dot(x, w_gate, preferred_element_type=jnp.float32)
        up = jnp.dot(x, w_up, preferred_element_type=jnp.float32)
        hidden = (jax.nn.silu(gate) * up).astype(jnp.bfloat16)
        term = jnp.dot(hidden, w_down, preferred_element_type=jnp.float32).astype(jnp.bfloat16)
        return lax.psum(term, "tp")

    return jax.shard_map(
        step,
        mesh=mesh,
        in_specs=(P("dp", None), P(None, "tp"), P(None, "tp"), P("tp", None)),
        out_specs=P("dp", None),
        check_vma=False,
    )
```

profile of v0, /device:TPU:0, one launch (start us, length us, event | category | flops | bytes accessed | tf_op | source)
XLA Modules:
  0.0 150.4 jit_solution(9332186536316541943)
XLA Ops:
  6.5 0.0 copy-start
  6.5 0.0 all-reduce.2.cloned.1.call-start
  6.5 1.6 %copy-done = bf16[128,8192]{1,0:T(8,128)(2,1)S(1)} copy-done((bf16[128,8192]{1,0:T(8,128)(2,1)S(1)}, bf16[128,8192]{1,0:T(8,128)(2,1)}, u32[]{:S(2)}) %copy-start) | copy-done | bytes 2097176
  8.1 21.3 %fusion.8 = f32[128,3584]{1,0:T(8,128)} fusion(bf16[128,8192]{1,0:T(8,128)(2,1)S(1)} %copy-done, bf16[8192,3584]{1,0:T(8,128)(2,1)} %param.5), kind=kOutput, calls=%fused_computation.10 | convolution fusion | flops 7516192768 | bytes 62652416 | tf_op jit(solution)/shard_map/dot_general | solution.py:9
  29.4 21.1 %fusion.clone.4 = bf16[128,3584]{1,0:T(8,128)(2,1)S(1)} fusion(bf16[128,8192]{1,0:T(8,128)(2,1)S(1)} %copy-done, bf16[8192,3584]{1,0:T(8,128)(2,1)} %param.6, f32[128,3584]{1,0:T(8,128)} %fusion.8), kind=kOutput, calls=%fused_computation.2.clone.clone.clone.1 | convolution fusion | flops 7518945280 | bytes 63569920 | tf_op jit(solution)/shard_map/dot_general | solution.py:10
  50.5 22.1 %convolution_convert_fusion = bf16[128,8192]{1,0:T(8,128)(2,1)} fusion(bf16[3584,8192]{1,0:T(8,128)(2,1)} %param.7, bf16[128,3584]{1,0:T(8,128)(2,1)S(1)} %fusion.clone.4), kind=kOutput, calls=%fused_computation | convolution fusion | flops 7517241344 | bytes 61734912 | tf_op jit(solution)/shard_map/dot_general | solution.py:12
  72.6 0.0 all-reduce.2.cloned.1.call-update
  72.6 0.0 copy-start.1
  72.6 67.8 %all-reduce.2.cloned.1.call-done = bf16[128,8192]{1,0:T(8,128)(2,1)} async-done(((bf16[128,8192]{1,0:T(8,128)(2,1)}), bf16[128,8192]{1,0:T(8,128)(2,1)}) %all-reduce.2.cloned.1.call-update) | async-done | bytes 2097168 | tf_op jit(solution)/shard_map/psum | solution.py:13
  140.4 3.1 %copy.6 = bf16[128,8192]{1,0:T(8,128)(2,1)} copy(bf16[128,8192]{1,0:T(8,128)(2,1)} %all-reduce.2.cloned.1.call-done) | data formatting | bytes 4194304
  143.5 0.0 copy-done.1
Async XLA Ops:
  6.5 1.6 %copy-start = (bf16[128,8192]{1,0:T(8,128)(2,1)S(1)}, bf16[128,8192]{1,0:T(8,128)(2,1)}, u32[]{:S(2)}) copy-start(bf16[128,8192]{1,0:T(8,128)(2,1)} %param.4) | copy-start | bytes 6291460
  6.5 133.9 %all-reduce.2.cloned.1.call-start = ((), (), s32[]{:S(2)}) async-start(), calls=%async_computation | async-start | bytes 4194304 | tf_op jit(solution)/shard_map/psum | solution.py:13
  72.6 70.9 %copy-start.1 = (bf16[128,8192]{1,0:T(8,128)(2,1)S(1)}, bf16[128,8192]{1,0:T(8,128)(2,1)}, u32[]{:S(2)}) copy-start(bf16[128,8192]{1,0:T(8,128)(2,1)} %param.4) | copy-start | bytes 6291460
Sparse Core Ops, SparseCore 0:
  72.7 67.6 all-reduce.1
where the time goes:
time: 151 us; the launch traced here: 150 us
  waiting for transfers between devices  67.8 us (45%)
  matrix products  64.5 us (43%)
  between operations  13.4 us (9%)
  local copies, waits for them, and re-layouts  4.69 us (3%)
    psum x1, waiting for transfers between devices, step(): return lax.psum(term, 'tp')  67.8 us
    dot_general x1, matrix products, step(): jnp.dot(hidden, w_down, preferred_element_type=jnp.float32)  22.1 us
    dot_general x1, matrix products, step(): gate = jnp.dot(x, w_gate, preferred_element_type=jnp.float32)  21.3 us
    dot_general x1, matrix products, step(): up = jnp.dot(x, w_up, preferred_element_type=jnp.float32)  21.1 us
    unnamed x5, local copies, waits for them, and re-layouts  4.69 us
  transfers between devices with their start and end apart: 1, of which 1 were waited for; matrix products, arithmetic and copies ran while one was open for 0% of the time, Pallas kernels for 0%

commit v1 on v0

v1 whole, which is shorter than its diff:
```python
import functools

import jax
import jax.numpy as jnp
from jax import lax
from jax.experimental import pallas as pl
from jax.experimental.pallas import tpu as pltpu
from jax.sharding import PartitionSpec as P

MESH = pl.DeviceIdType.MESH
FC = 256
A_DEPTH = 3
YC = 512
B_DEPTH = 4
LAG_Z1, LAG_Z2, LAG_Z3, LAG_DONE = 4, 7, 9, 10


def kernel(
    x_hbm, wg_hbm, wu_hbm, wd_hbm, y_hbm,
    x, hidden, wg, wu, wd, own, core_out, core_in, z_out, z_in1, z_in2, y,
    x_sem, wg_sem, wu_sem, wd_sem, y_sem,
    core_ss, core_rs, z1_ss, z1_rs, z2_ss, z2_rs, z3_ss, z3_rs, fin_ss, fin_rs,
):
    rows, depth = x.shape
    half = rows // 2
    na = hidden.shape[0]
    nb = y.shape[0]
    dp = lax.axis_index("dp")
    tp = lax.axis_index("tp")
    chip = tp // 2
    core = tp % 2
    partner = (dp, tp + 1 - 2 * core)
    pair = (dp, tp + 2 - 4 * (chip % 2))
    cross = (dp, 2 * (3 - chip) + core)
    outer = (chip == 0) | (chip == 3)
    inner = jnp.logical_not(outer)
    mine = pl.ds(pl.multiple_of(core * half, half), half)
    theirs = pl.ds(pl.multiple_of((1 - core) * half, half), half)

    def load_a(w_hbm, buf, sem, i):
        slot = lax.rem(i, A_DEPTH)
        cols = pl.ds(pl.multiple_of(i * FC, FC), FC)
        return pltpu.make_async_copy(w_hbm.at[:, cols], buf.at[slot], sem.at[slot])

    def load_b(i):
        slot = lax.rem(i, B_DEPTH)
        cols = pl.ds(pl.multiple_of(i * YC, YC), YC)
        return pltpu.make_async_copy(wd_hbm.at[:, cols], wd.at[slot], wd_sem.at[slot])

    def store_y(c):
        cols = pl.ds(pl.multiple_of(c * YC, YC), YC)
        return pltpu.make_async_copy(y.at[c], y_hbm.at[:, cols], y_sem.at[c])

    def remote(src, dst, ss, rs, c, to):
        return pltpu.make_async_remote_copy(
            src_ref=src, dst_ref=dst, send_sem=ss.at[c], recv_sem=rs.at[c],
            device_id=to, device_id_type=MESH,
        )

    def to_core(c):
        return remote(core_out.at[c], core_in.at[c], core_ss, core_rs, c, partner)

    def to_inner(c):
        return remote(z_out.at[c], z_in1.at[c], z1_ss, z1_rs, c, pair)

    def to_cross(c):
        return remote(z_out.at[c], z_in2.at[c], z2_ss, z2_rs, c, cross)

    def to_outer(c):
        return remote(y.at[c, mine], y.at[c, mine], z3_ss, z3_rs, c, pair)

    def to_partner(c):
        return remote(y.at[c, mine], y.at[c, mine], fin_ss, fin_rs, c, partner)

    def from_partner(c):
        return remote(y.at[c, theirs], y.at[c, theirs], fin_ss, fin_rs, c, partner)

    x_copy = pltpu.make_async_copy(x_hbm, x, x_sem)
    x_copy.start()
    for i in range(A_DEPTH):
        load_a(wg_hbm, wg, wg_sem, i).start()
        load_a(wu_hbm, wu, wu_sem, i).start()

    barrier = pltpu.get_barrier_semaphore()
    pl.semaphore_signal(barrier, inc=1, device_id=partner, device_id_type=MESH)
    pl.semaphore_signal(barrier, inc=1, device_id=pair, device_id_type=MESH)

    @pl.when(inner)
    def _():
        pl.semaphore_signal(barrier, inc=1, device_id=cross, device_id_type=MESH)

    x_copy.wait()

    def step_a(i, _):
        slot = lax.rem(i, A_DEPTH)
        load_a(wg_hbm, wg, wg_sem, i).wait()
        gate = jnp.dot(x[...], wg[slot], preferred_element_type=jnp.float32)
        load_a(wu_hbm, wu, wu_sem, i).wait()
        up = jnp.dot(x[...], wu[slot], preferred_element_type=jnp.float32)
        hidden[i] = (jax.nn.silu(gate) * up).astype(jnp.bfloat16)

        @pl.when(i + A_DEPTH < na)
        def _():
            load_a(wg_hbm, wg, wg_sem, i + A_DEPTH).start()
            load_a(wu_hbm, wu, wu_sem, i + A_DEPTH).start()

        later = i + A_DEPTH - na

        @pl.when((later >= 0) & (later < B_DEPTH))
        def _():
            load_b(later).start()

        return 0

    lax.fori_loop(0, na, step_a, 0)
    for i in range(A_DEPTH, B_DEPTH):
        load_b(i).start()

    @pl.when(outer)
    def _():
        pl.semaphore_wait(barrier, 2)

    @pl.when(inner)
    def _():
        pl.semaphore_wait(barrier, 3)

    def step_b(j, _):
        @pl.when(j < nb)
        def _():
            slot = lax.rem(j, B_DEPTH)
            load_b(j).wait()
            term = jnp.zeros((rows, YC), jnp.float32)
            for k in range(na):
                term += jnp.dot(
                    hidden[k], wd[slot, k * FC:(k + 1) * FC, :],
                    preferred_element_type=jnp.float32,
                )

            @pl.when(core == 0)
            def _():
                own[j] = term[:half]
                core_out[j] = term[half:].astype(jnp.bfloat16)

            @pl.when(core == 1)
            def _():
                own[j] = term[half:]
                core_out[j] = term[:half].astype(jnp.bfloat16)

            to_core(j).start()

            @pl.when(j + B_DEPTH < nb)
            def _():
                load_b(j + B_DEPTH).start()

        c1 = j - 1

        @pl.when((c1 >= 0) & (c1 < nb))
        def _():
            to_core(c1).wait_recv()
            total = own[c1] + core_in[c1].astype(jnp.float32)

            @pl.when(outer)
            def _():
                z_out[c1] = total.astype(jnp.bfloat16)
                to_inner(c1).start()

            @pl.when(inner)
            def _():
                own[c1] = total

        c2 = j - LAG_Z1

        @pl.when(inner & (c2 >= 0) & (c2 < nb))
        def _():
            to_inner(c2).wait_recv()
            z_out[c2] = (own[c2] + z_in1[c2].astype(jnp.float32)).astype(jnp.bfloat16)
            to_cross(c2).start()

        c3 = j - LAG_Z2

        @pl.when(inner & (c3 >= 0) & (c3 < nb))
        def _():
            to_cross(c3).wait_recv()
            y[c3, mine] = (
                z_out[c3].astype(jnp.float32) + z_in2[c3].astype(jnp.float32)
            ).astype(jnp.bfloat16)
            to_outer(c3).start()
            to_partner(c3).start()

        c4 = j - LAG_Z3

        @pl.when(outer & (c4 >= 0) & (c4 < nb))
        def _():
            to_outer(c4).wait_recv()
            to_partner(c4).start()

        c5 = j - LAG_DONE

        @pl.when((c5 >= 0) & (c5 < nb))
        def _():
            from_partner(c5).wait_recv()
            store_y(c5).start()

        return 0

    lax.fori_loop(0, nb + LAG_DONE, step_b, 0)

    def drain(c, _):
        store_y(c).wait()
        to_core(c).wait_send()
        to_partner(c).wait_send()

        @pl.when(outer)
        def _():
            to_inner(c).wait_send()

        @pl.when(inner)
        def _():
            to_cross(c).wait_send()
            to_outer(c).wait_send()

        return 0

    lax.fori_loop(0, nb, drain, 0)


def solution(mesh):
    def step(x, w_gate, w_up, w_down):
        rows, depth = x.shape
        ff = w_gate.shape[1]
        half = rows // 2
        na, nb = ff // FC, depth // YC
        bf16, f32 = jnp.bfloat16, jnp.float32
        hbm = pl.BlockSpec(memory_space=pltpu.HBM)
        dma = pltpu.SemaphoreType.DMA
        return pl.pallas_call(
            kernel,
            out_shape=jax.ShapeDtypeStruct((rows, depth), bf16),
            in_specs=[hbm] * 4,
            out_specs=hbm,
            scratch_shapes=[
                pltpu.VMEM((rows, depth), bf16),
                pltpu.VMEM((na, rows, FC), bf16),
                pltpu.VMEM((A_DEPTH, depth, FC), bf16),
                pltpu.VMEM((A_DEPTH, depth, FC), bf16),
                pltpu.VMEM((B_DEPTH, ff, YC), bf16),
                pltpu.VMEM((nb, half, YC), f32),
                pltpu.VMEM((nb, half, YC), bf16),
                pltpu.VMEM((nb, half, YC), bf16),
                pltpu.VMEM((nb, half, YC), bf16),
                pltpu.VMEM((nb, half, YC), bf16),
                pltpu.VMEM((nb, half, YC), bf16),
                pltpu.VMEM((nb, rows, YC), bf16),
                dma, dma((A_DEPTH,)), dma((A_DEPTH,)), dma((B_DEPTH,)), dma((nb,)),
            ] + [dma((nb,))] * 10,
            compiler_params=pltpu.CompilerParams(
                collective_id=0, has_side_effects=True, vmem_limit_bytes=64 * 1024 * 1000
            ),
            cost_estimate=pl.CostEstimate(
                flops=6 * rows * depth * ff, bytes_accessed=6 * depth * ff, transcendentals=rows * ff
            ),
        )(x, w_gate, w_up, w_down)

    return jax.shard_map(
        step,
        mesh=mesh,
        in_specs=(P("dp", None), P(None, "tp"), P(None, "tp"), P("tp", None)),
        out_specs=P("dp", None),
        check_vma=False,
    )
```

time: 151 us -> 83.6 us (0.55)
  Pallas kernels: 0 us -> 79.9 us
  waiting for transfers between devices: 67.8 us -> 0 us
  matrix products: 64.5 us -> 0 us
  between operations: 13.4 us -> 0.01 us
  local copies, waits for them, and re-layouts: 4.69 us -> 3.1 us
    pallas_call x0 -> x1, Pallas kernels: none -> 79.9 us  [step(): pl.pallas_call(kernel, out_shape=jax.ShapeDtypeStruct((rows, depth), bf16...]
    psum x1 -> x0, waiting for transfers between devices: 67.8 us -> none  [step(): return lax.psum(term, 'tp')]
    dot_general x3 -> x0, matrix products: 64.5 us -> none  [the longest x1 22.1 us: step(): jnp.dot(hidden, w_down, preferred_element_type=jnp.float32)]
    unnamed x5 -> x1, local copies, waits for them, and re-layouts: 4.69 us -> 3.1 us
  transfers between devices with their start and end apart: 1 -> 0, of which waited for: 1 -> 0; matrix products, arithmetic and copies ran while one was open for 0% -> 0% of each run, Pallas kernels for 0% -> 0%
where the time goes in v1:
time: 83.6 us; the launch traced here: 83 us
  Pallas kernels  79.9 us (96%)
  local copies, waits for them, and re-layouts  3.1 us (4%)
    pallas_call x1, Pallas kernels, step(): pl.pallas_call(kernel, out_shape=jax.ShapeDtypeStruct((rows, depth), bf16...  79.9 us
    unnamed x1, local copies, waits for them, and re-layouts  3.1 us

profile of v1, /device:TPU:0, one launch (start us, length us, event | category | flops | bytes accessed | tf_op | source)
XLA Modules:
  0.0 83.0 jit_solution(9595785434640295827)
XLA Ops:
  0.0 79.9 %shard_map.46 = bf16[128,8192]{1,0:T(8,128)(2,1)} custom-call(bf16[128,8192]{1,0:T(8,128)(2,1)} %x_hbm.1, bf16[8192,3584]{1,0:T(8,128)(2,1)} %wg_hbm.1, bf16[8192,3584]{1,0:T(8,128)(2,1)} %wu_hbm.1, bf16[3584,8192]{1,0:T(8,128)(2,1)} %wd_hbm.1), custom_call_target="tpu_custom_call" | custom-call | flops 22548578304 | bytes 176160768 | tf_op jit(solution)/shard_map/pallas_call | solution.py:236
  79.9 3.1 %copy.6 = bf16[128,8192]{1,0:T(8,128)(2,1)} copy(bf16[128,8192]{1,0:T(8,128)(2,1)} %shard_map.46) | data formatting | bytes 4194304

commit v2 on v1

v2 whole, which is shorter than its diff:
```python
import functools

import jax
import jax.numpy as jnp
from jax import lax
from jax.experimental import pallas as pl
from jax.experimental.pallas import tpu as pltpu
from jax.sharding import PartitionSpec as P

MESH = pl.DeviceIdType.MESH
FC = 256
YC = 512
NBUF = 8
W = 2
SHARED = 0
FIRST = 5
LAG_NB = 2
PIECES = 8
X0, Z0 = 1, 4
LAG_C, LAG_Z1, LAG_Z2, LAG_Z3 = 1, 4, 7, 9
B_PRIORITY = 0


def kernel(
    x_hbm, wg_hbm, wu_hbm, wd_hbm, y,
    xx, hidden, sent, ring, own, core_out, core_in, z_out, z_in1, z_in2,
    x_sem, ring_sem,
    core_ss, core_rs, z1_ss, z1_rs, z2_ss, z2_rs, z3_ss, z3_rs, fin_ss, fin_rs,
    xa_ss, xa_rs, xz_ss, xz_rs, xc_ss, xc_rs, xd_ss, xd_rs, h_ss, h_rs,
):
    rows, depth = x_hbm.shape
    half = rows // 2
    na = hidden.shape[0]
    nb = depth // YC
    ff = na * FC
    plain = na - 2 * SHARED
    first = min(FIRST, plain)
    loads = plain + SHARED
    quarter = depth // 4
    width = quarter // PIECES

    dp = lax.axis_index("dp")
    tp = lax.axis_index("tp")
    chip = tp // 2
    core = tp % 2
    side = dp // 2
    partner = (dp, tp + 1 - 2 * core)
    pair = (dp, tp + 2 - 4 * (chip % 2))
    cross = (dp, 2 * (3 - chip) + core)
    twin = ((dp + 2) % 4, tp)
    outer = (chip == 0) | (chip == 3)
    inner = jnp.logical_not(outer)
    mine = pl.ds(pl.multiple_of(core * half, half), half)
    theirs = pl.ds(pl.multiple_of((1 - core) * half, half), half)

    def chunk(i):
        shared = plain + 2 * (i - first) + side
        return jnp.where(i < first, i, jnp.where(i < first + SHARED, shared, i - SHARED))

    def load_a(w_hbm, i, which):
        slot = lax.rem(2 * i + which, NBUF)
        cols = pl.ds(pl.multiple_of(chunk(i) * FC, FC), FC)
        return pltpu.make_async_copy(w_hbm.at[:, cols], ring.at[slot], ring_sem.at[slot, 0])

    def load_b(j):
        slot = lax.rem(2 * loads + j, NBUF)
        return [
            pltpu.make_async_copy(
                wd_hbm.at[:, pl.ds(pl.multiple_of(j * YC + p * FC, FC), FC)],
                ring.at[slot, pl.ds(p * ff, ff)],
                ring_sem.at[slot, p],
            )
            for p in range(YC // FC)
        ]

    def start_b(j):
        for copy in load_b(j):
            copy.start(priority=B_PRIORITY)

    def start_item(i, which):
        @pl.when(i < loads)
        def _():
            load_a(wu_hbm if which else wg_hbm, i, which).start()

        @pl.when((i >= loads) & (2 * (i - loads) + which < nb))
        def _():
            start_b(2 * (i - loads) + which)

    def remote(src, dst, ss, rs, c, to):
        return pltpu.make_async_remote_copy(
            src_ref=src, dst_ref=dst, send_sem=ss.at[c], recv_sem=rs.at[c],
            device_id=to, device_id_type=MESH,
        )

    def ycols(c):
        return pl.ds(pl.multiple_of(c * YC, YC), YC)

    def to_core(c):
        return remote(core_out.at[c], core_in.at[c], core_ss, core_rs, c, partner)

    def to_inner(c):
        return remote(z_out.at[c], z_in1.at[c], z1_ss, z1_rs, c, pair)

    def to_cross(c):
        return remote(z_out.at[c], z_in2.at[c], z2_ss, z2_rs, c, cross)

    def to_outer(c):
        part = y.at[mine, ycols(c)]
        return remote(part, part, z3_ss, z3_rs, c, pair)

    def to_partner(c):
        part = y.at[mine, ycols(c)]
        return remote(part, part, fin_ss, fin_rs, c, partner)

    def from_partner(c):
        part = y.at[theirs, ycols(c)]
        return remote(part, part, fin_ss, fin_rs, c, partner)

    def piece(z, c, k):
        return pl.ds(pl.multiple_of((2 * z + c) * quarter + k * width, width), width)

    zpar = chip % 2

    def x_to_twin(k):
        cols = piece(zpar, core, k)
        return remote(xx.at[0, :, cols], xx.at[1, :, cols], xa_ss, xa_rs, k, twin)

    def x_to_pair(k):
        part = xx.at[1, :, piece(zpar, core, k)]
        return remote(part, part, xz_ss, xz_rs, k, pair)

    def x_from_pair(k):
        part = xx.at[1, :, piece(1 - zpar, core, k)]
        return remote(part, part, xz_ss, xz_rs, k, pair)

    def x_to_core(k):
        part = xx.at[1, :, piece(zpar, core, k)]
        return remote(part, part, xc_ss, xc_rs, k, partner)

    def x_from_core(k):
        part = xx.at[1, :, piece(zpar, 1 - core, k)]
        return remote(part, part, xc_ss, xc_rs, k, partner)

    def xz_to_core(k):
        part = xx.at[1, :, piece(1 - zpar, core, k)]
        return remote(part, part, xd_ss, xd_rs, k, partner)

    def xz_from_core(k):
        part = xx.at[1, :, piece(1 - zpar, 1 - core, k)]
        return remote(part, part, xd_ss, xd_rs, k, partner)

    def h_to_twin(t):
        there = hidden.at[plain + 2 * t + side]
        return remote(sent.at[t], there, h_ss, h_rs, t, twin)

    def h_from_twin(t):
        here = hidden.at[plain + 2 * t + 1 - side]
        return remote(sent.at[t], here, h_ss, h_rs, t, twin)

    def forward(s):
        if not SHARED:
            return
        kx = s - X0

        @pl.when((kx >= 0) & (kx < PIECES))
        def _():
            x_to_twin(kx).wait_recv()
            x_to_pair(kx).start()
            x_to_core(kx).start()

        kz = s - Z0

        @pl.when((kz >= 0) & (kz < PIECES))
        def _():
            x_from_pair(kz).wait_recv()
            xz_to_core(kz).start()

    x_copies = [
        pltpu.make_async_copy(
            x_hbm.at[:, pl.ds(q * quarter, quarter)],
            xx.at[0, :, pl.ds(q * quarter, quarter)],
            x_sem.at[q],
        )
        for q in range(4)
    ]
    for copy in x_copies:
        copy.start()
    for i in range(W // 2):
        load_a(wg_hbm, i, 0).start()
        load_a(wu_hbm, i, 1).start()

    barrier = pltpu.get_barrier_semaphore()
    peers = [partner, pair] + ([twin] if SHARED else [])
    for peer in peers:
        pl.semaphore_signal(barrier, inc=1, device_id=peer, device_id_type=MESH)

    @pl.when(inner)
    def _():
        pl.semaphore_signal(barrier, inc=1, device_id=cross, device_id_type=MESH)

    for copy in x_copies:
        copy.wait()

    def meet():
        @pl.when(outer)
        def _():
            pl.semaphore_wait(barrier, len(peers))

        @pl.when(inner)
        def _():
            pl.semaphore_wait(barrier, len(peers) + 1)

    if SHARED:
        meet()
    if SHARED:
        for k in range(PIECES):
            x_to_twin(k).start()

    def gated(gate, up):
        return (jax.nn.silu(gate) * up).astype(jnp.bfloat16)

    def step_a(i, _):
        if SHARED:
            n = i - LAG_NB
            t = n - first

            @pl.when(t == 0)
            def _():
                def arrive(k, _):
                    x_from_core(k).wait_recv()
                    xz_from_core(k).wait_recv()
                    return 0

                lax.fori_loop(0, PIECES, arrive, 0)

            @pl.when((t >= 0) & (t < SHARED))
            def _():
                slot = lax.rem(2 * n, NBUF)
                gate = jnp.dot(xx[1], ring[slot], preferred_element_type=jnp.float32)
                up = jnp.dot(xx[1], ring[slot + 1], preferred_element_type=jnp.float32)
                sent[t] = gated(gate, up)
                h_to_twin(t).start()

        @pl.when(i < loads)
        def _():
            slot = lax.rem(2 * i, NBUF)
            forward(2 * i)
            load_a(wg_hbm, i, 0).wait()
            start_item(i + W // 2, 0)
            gate = jnp.dot(xx[0], ring[slot], preferred_element_type=jnp.float32)
            forward(2 * i + 1)
            load_a(wu_hbm, i, 1).wait()
            start_item(i + W // 2, 1)
            up = jnp.dot(xx[0], ring[slot + 1], preferred_element_type=jnp.float32)
            hidden[chunk(i)] = gated(gate, up)

        return 0

    extra = max(0, first + SHARED + LAG_NB - loads) if SHARED else 0
    lax.fori_loop(0, loads + extra, step_a, 0)
    if not SHARED:
        meet()
    for t in range(SHARED):
        h_from_twin(t).wait_recv()

    def step_b(j, _):
        @pl.when(j < nb)
        def _():
            slot = lax.rem(2 * loads + j, NBUF)
            for copy in load_b(j):
                copy.wait()

            @pl.when(j + W < nb)
            def _():
                start_b(j + W)

            terms = [jnp.zeros((rows, FC), jnp.float32) for _ in range(YC // FC)]
            for k in range(na):
                for p in range(YC // FC):
                    at = p * ff + k * FC
                    terms[p] += jnp.dot(
                        hidden[k], ring[slot, at:at + FC, :],
                        preferred_element_type=jnp.float32,
                    )
            for p, term in enumerate(terms):
                cols = pl.ds(p * FC, FC)

                @pl.when(core == 0)
                def _():
                    own[j, :, cols] = term[:half]
                    core_out[j, :, cols] = term[half:].astype(jnp.bfloat16)

                @pl.when(core == 1)
                def _():
                    own[j, :, cols] = term[half:]
                    core_out[j, :, cols] = term[:half].astype(jnp.bfloat16)

            to_core(j).start()

        c1 = j - LAG_C

        @pl.when((c1 >= 0) & (c1 < nb))
        def _():
            to_core(c1).wait_recv()
            total = own[c1] + core_in[c1].astype(jnp.float32)

            @pl.when(outer)
            def _():
                z_out[c1] = total.astype(jnp.bfloat16)
                to_inner(c1).start()

            @pl.when(inner)
            def _():
                own[c1] = total

        c2 = j - LAG_Z1

        @pl.when(inner & (c2 >= 0) & (c2 < nb))
        def _():
            to_inner(c2).wait_recv()
            z_out[c2] = (own[c2] + z_in1[c2].astype(jnp.float32)).astype(jnp.bfloat16)
            to_cross(c2).start()

        c3 = j - LAG_Z2

        @pl.when(inner & (c3 >= 0) & (c3 < nb))
        def _():
            to_cross(c3).wait_recv()
            y[mine, ycols(c3)] = (
                z_out[c3].astype(jnp.float32) + z_in2[c3].astype(jnp.float32)
            ).astype(jnp.bfloat16)
            to_outer(c3).start()
            to_partner(c3).start()

        c4 = j - LAG_Z3

        @pl.when(outer & (c4 >= 0) & (c4 < nb))
        def _():
            to_outer(c4).wait_recv()
            to_partner(c4).start()

        return 0

    lax.fori_loop(0, nb + LAG_Z3, step_b, 0)

    def drain(c, _):
        to_core(c).wait_send()
        to_partner(c).wait_send()
        from_partner(c).wait_recv()

        @pl.when(outer)
        def _():
            to_inner(c).wait_send()

        @pl.when(inner)
        def _():
            to_cross(c).wait_send()
            to_outer(c).wait_send()

        return 0

    lax.fori_loop(0, nb, drain, 0)
    if SHARED:
        def drain_x(k, _):
            x_to_twin(k).wait_send()
            x_to_pair(k).wait_send()
            x_to_core(k).wait_send()
            xz_to_core(k).wait_send()
            return 0

        lax.fori_loop(0, PIECES, drain_x, 0)
        for t in range(SHARED):
            h_to_twin(t).wait_send()


def solution(mesh):
    def step(x, w_gate, w_up, w_down):
        rows, depth = x.shape
        ff = w_gate.shape[1]
        half = rows // 2
        na, nb = ff // FC, depth // YC
        bf16, f32 = jnp.bfloat16, jnp.float32
        hbm = pl.BlockSpec(memory_space=pltpu.HBM)
        dma = pltpu.SemaphoreType.DMA
        slots = max(SHARED, 1)
        return pl.pallas_call(
            kernel,
            out_shape=jax.ShapeDtypeStruct((rows, depth), bf16),
            in_specs=[hbm] * 4,
            out_specs=pl.BlockSpec(memory_space=pltpu.VMEM),
            scratch_shapes=[
                pltpu.VMEM((2, rows, depth), bf16),
                pltpu.VMEM((na, rows, FC), bf16),
                pltpu.VMEM((slots, rows, FC), bf16),
                pltpu.VMEM((NBUF, depth, FC), bf16),
                pltpu.VMEM((nb, half, YC), f32),
            ] + [pltpu.VMEM((nb, half, YC), bf16)] * 5 + [
                dma((4,)), dma((NBUF, 2)),
            ] + [dma((nb,))] * 10 + [dma((PIECES,))] * 8 + [dma((slots,))] * 2,
            compiler_params=pltpu.CompilerParams(
                collective_id=0, has_side_effects=True, vmem_limit_bytes=50 * 1024 * 1024
            ),
            cost_estimate=pl.CostEstimate(
                flops=6 * rows * depth * ff, bytes_accessed=6 * depth * ff, transcendentals=rows * ff
            ),
        )(pltpu.with_memory_space_constraint(x, pltpu.HBM), w_gate, w_up, w_down)

    return jax.shard_map(
        step,
        mesh=mesh,
        in_specs=(P("dp", None), P(None, "tp"), P(None, "tp"), P("tp", None)),
        out_specs=P("dp", None),
        check_vma=False,
    )
```

time: 83.6 us -> 79.5 us (0.951)
  Pallas kernels: 79.9 us -> 78 us
  local copies, waits for them, and re-layouts: 3.1 us -> 1.32 us
    pallas_call x1, Pallas kernels: 79.9 us -> 78 us  [step(): pl.pallas_call(kernel, out_shape=jax.ShapeDtypeStruct((rows, depth), bf16...]
    unnamed x1, local copies, waits for them, and re-layouts: 3.1 us -> 1.32 us
where the time goes in v2:
time: 79.5 us; the launch traced here: 79.4 us
  Pallas kernels  78 us (98%)
  local copies, waits for them, and re-layouts  1.32 us (2%)
    pallas_call x1, Pallas kernels, step(): pl.pallas_call(kernel, out_shape=jax.ShapeDtypeStruct((rows, depth), bf16...  78 us

profile of v2, /device:TPU:0, one launch (start us, length us, event | category | flops | bytes accessed | tf_op | source)
XLA Modules:
  0.0 79.4 jit_solution(15659111424776689219)
XLA Ops:
  0.0 78.0 %shard_map.46 = bf16[128,8192]{1,0:T(8,128)(2,1)S(1)} custom-call(bf16[128,8192]{1,0:T(8,128)(2,1)} %x_hbm.1, bf16[8192,3584]{1,0:T(8,128)(2,1)} %wg_hbm.1, bf16[8192,3584]{1,0:T(8,128)(2,1)} %wu_hbm.1, bf16[3584,8192]{1,0:T(8,128)(2,1)} %wd_hbm.1), custom_call_target="tpu_custom_call" | custom-call | flops 22548578304 | bytes 176160768 | tf_op jit(solution)/shard_map/pallas_call | solution.py:386
  78.0 1.3 %copy.6 = bf16[128,8192]{1,0:T(8,128)(2,1)} copy(bf16[128,8192]{1,0:T(8,128)(2,1)S(1)} %shard_map.46) | data formatting | bytes 4194304

commit v3 on v2

--- a/solution.py
+++ b/solution.py
@@ -11,14 +11,14 @@
 FC = 256
 YC = 512
 NBUF = 8
-W = 2
-SHARED = 0
-FIRST = 5
+W = 4
+SHARED = 2
+FIRST = 7
 LAG_NB = 2
 PIECES = 8
-X0, Z0 = 1, 4
+X0, Z0 = 6, 9
 LAG_C, LAG_Z1, LAG_Z2, LAG_Z3 = 1, 4, 7, 9
-B_PRIORITY = 0
+B_PRIORITY = 1
 
 
 def kernel(
@@ -80,7 +80,7 @@
     def start_item(i, which):
         @pl.when(i < loads)
         def _():
-            load_a(wu_hbm if which else wg_hbm, i, which).start()
+            load_a(wu_hbm if which else wg_hbm, i, which).start(priority=1)
 
         @pl.when((i >= loads) & (2 * (i - loads) + which < nb))
         def _():
@@ -185,9 +185,8 @@
     ]
     for copy in x_copies:
         copy.start()
-    for i in range(W // 2):
-        load_a(wg_hbm, i, 0).start()
-        load_a(wu_hbm, i, 1).start()
+    for n in range(W):
+        load_a(wu_hbm if n % 2 else wg_hbm, n // 2, n % 2).start(priority=1)
 
     barrier = pltpu.get_barrier_semaphore()
     peers = [partner, pair] + ([twin] if SHARED else [])
@@ -246,11 +245,11 @@
             slot = lax.rem(2 * i, NBUF)
             forward(2 * i)
             load_a(wg_hbm, i, 0).wait()
-            start_item(i + W // 2, 0)
+            start_item(i + W // 2, W % 2)
             gate = jnp.dot(xx[0], ring[slot], preferred_element_type=jnp.float32)
             forward(2 * i + 1)
             load_a(wu_hbm, i, 1).wait()
-            start_item(i + W // 2, 1)
+            start_item(i + (W + 1) // 2, 1 - W % 2)
             up = jnp.dot(xx[0], ring[slot + 1], preferred_element_type=jnp.float32)
             hidden[chunk(i)] = gated(gate, up)
 
@@ -313,14 +312,6 @@
             def _():
                 own[c1] = total
 
-        c2 = j - LAG_Z1
-
-        @pl.when(inner & (c2 >= 0) & (c2 < nb))
-        def _():
-            to_inner(c2).wait_recv()
-            z_out[c2] = (own[c2] + z_in1[c2].astype(jnp.float32)).astype(jnp.bfloat16)
-            to_cross(c2).start()
-
         c3 = j - LAG_Z2
 
         @pl.when(inner & (c3 >= 0) & (c3 < nb))
@@ -331,6 +322,14 @@
             ).astype(jnp.bfloat16)
             to_outer(c3).start()
             to_partner(c3).start()
+
+        c2 = j - LAG_Z1
+
+        @pl.when(inner & (c2 >= 0) & (c2 < nb))
+        def _():
+            to_inner(c2).wait_recv()
+            z_out[c2] = (own[c2] + z_in1[c2].astype(jnp.float32)).astype(jnp.bfloat16)
+            to_cross(c2).start()
 
         c4 = j - LAG_Z3
 

time: 79.5 us -> 77.4 us (0.974)
  Pallas kernels: 78 us -> 75.9 us
    pallas_call x1, Pallas kernels: 78 us -> 75.9 us  [step(): pl.pallas_call(kernel, out_shape=jax.ShapeDtypeStruct((rows, depth), bf16...]
where the time goes in v3:
time: 77.4 us; the launch traced here: 77.3 us
  Pallas kernels  75.9 us (98%)
  local copies, waits for them, and re-layouts  1.32 us (2%)
    pallas_call x1, Pallas kernels, step(): pl.pallas_call(kernel, out_shape=jax.ShapeDtypeStruct((rows, depth), bf16...  75.9 us

profile of v3, /device:TPU:0, one launch (start us, length us, event | category | flops | bytes accessed | tf_op | source)
XLA Modules:
  0.0 77.3 jit_solution(7056160718738933037)
XLA Ops:
  0.0 75.9 %shard_map.46 = bf16[128,8192]{1,0:T(8,128)(2,1)S(1)} custom-call(bf16[128,8192]{1,0:T(8,128)(2,1)} %x_hbm.1, bf16[8192,3584]{1,0:T(8,128)(2,1)} %wg_hbm.1, bf16[8192,3584]{1,0:T(8,128)(2,1)} %wu_hbm.1, bf16[3584,8192]{1,0:T(8,128)(2,1)} %wd_hbm.1), custom_call_target="tpu_custom_call" | custom-call | flops 22548578304 | bytes 176160768 | tf_op jit(solution)/shard_map/pallas_call | solution.py:385
  75.9 1.3 %copy.6 = bf16[128,8192]{1,0:T(8,128)(2,1)} copy(bf16[128,8192]{1,0:T(8,128)(2,1)S(1)} %shard_map.46) | data formatting | bytes 4194304

commit v4 on v3

--- a/solution.py
+++ b/solution.py
@@ -12,8 +12,8 @@
 YC = 512
 NBUF = 8
 W = 4
-SHARED = 2
-FIRST = 7
+SHARED = 1
+FIRST = 8
 LAG_NB = 2
 PIECES = 8
 X0, Z0 = 6, 9

time: 77.4 us -> 78.7 us (1.017)
  Pallas kernels: 75.9 us -> 77.2 us
    pallas_call x1, Pallas kernels: 75.9 us -> 77.2 us  [step(): pl.pallas_call(kernel, out_shape=jax.ShapeDtypeStruct((rows, depth), bf16...]
where the time goes in v4:
time: 78.7 us; the launch traced here: 78.6 us
  Pallas kernels  77.2 us (98%)
  local copies, waits for them, and re-layouts  1.32 us (2%)
    pallas_call x1, Pallas kernels, step(): pl.pallas_call(kernel, out_shape=jax.ShapeDtypeStruct((rows, depth), bf16...  77.2 us

profile of v4, /device:TPU:0, one launch (start us, length us, event | category | flops | bytes accessed | tf_op | source)
XLA Modules:
  0.0 78.6 jit_solution(17435178727653735582)
XLA Ops:
  0.0 77.2 %shard_map.46 = bf16[128,8192]{1,0:T(8,128)(2,1)S(1)} custom-call(bf16[128,8192]{1,0:T(8,128)(2,1)} %x_hbm.1, bf16[8192,3584]{1,0:T(8,128)(2,1)} %wg_hbm.1, bf16[8192,3584]{1,0:T(8,128)(2,1)} %wu_hbm.1, bf16[3584,8192]{1,0:T(8,128)(2,1)} %wd_hbm.1), custom_call_target="tpu_custom_call" | custom-call | flops 22548578304 | bytes 176160768 | tf_op jit(solution)/shard_map/pallas_call | solution.py:385
  77.2 1.3 %copy.6 = bf16[128,8192]{1,0:T(8,128)(2,1)} copy(bf16[128,8192]{1,0:T(8,128)(2,1)S(1)} %shard_map.46) | data formatting | bytes 4194304
